TPU v7x, 32 devices: a whole 2x2x4 slice. The times are simulated.
32 devices in a mesh: row: 8 (over z, y), col: 4 (over x, core).
Axes of the slice: x: 2, y: 2, z: 4, core: 2. Of those that a mesh axis runs over, the one named last changes fastest.
Arguments:
- densities: bfloat16 [4608, 3072], P(('row', 'col')), may hold values from -0.796875 to 0.796875
- counts: int32 [512], P(('row', 'col')), may hold values from 3 to 9
- coulomb: float32 [3072], replicated, may hold values from 0.05 to 1
- energies: float32 [4608], P(('row', 'col')), may hold values from 8 to 64
- vectors: bfloat16 [4608, 64], P(('row', 'col')), may hold values from -0.09375 to 0.09375
Outputs:
- kernel: float32 [4608, 4608], P('row', 'col')
- product: float32 [4608, 64], P(('row', 'col'))
All inputs are finite; a program needn't handle non-finite values.
Results may differ from a plain program's by a relative error of at most 0.0095.
Values may be sent and summed in bfloat16 or wider, within the bound.
A program may use at most 128 MiB of HBM per device.

v0:
```python
import jax
import jax.numpy as jnp
from jax import lax
from jax.sharding import PartitionSpec as P

SLOT = 9


def body(densities, counts, coulomb, energies, vectors):
    kpoints = counts.shape[0]
    slot_index = lax.broadcasted_iota(jnp.int32, (kpoints, SLOT), 1)
    usable = (slot_index < counts[:, None]).reshape(kpoints * SLOT)
    masked = jnp.where(usable[:, None], densities, jnp.zeros_like(densities))
    weighted = (masked.astype(jnp.float32) * coulomb[None, :]).astype(jnp.bfloat16)
    row_block = lax.all_gather(weighted, "col", axis=0, tiled=True)
    kernel = lax.dot_general(
        row_block,
        lax.all_gather(masked, "row", axis=0, tiled=True),
        (((1,), (1,)), ((), ())),
        preferred_element_type=jnp.float32,
    )
    local_terms = lax.dot_general(
        masked, vectors, (((0,), (0,)), ((), ())), preferred_element_type=jnp.float32
    )
    projected = lax.psum(local_terms, ("row", "col"))
    coupled = jnp.dot(
        weighted.astype(jnp.float32),
        projected,
        precision=lax.Precision.HIGHEST,
        preferred_element_type=jnp.float32,
    )
    diagonal = jnp.where(usable, energies, jnp.zeros_like(energies))
    product = coupled + diagonal[:, None] * vectors.astype(jnp.float32)
    return (kernel, product)


def solution(mesh):
    return jax.shard_map(
        body,
        mesh=mesh,
        in_specs=(
            P(("row", "col"), None),
            P(("row", "col")),
            P(),
            P(("row", "col")),
            P(("row", "col"), None),
        ),
        out_specs=(P("row", "col"), P(("row", "col"), None)),
        check_vma=False,
    )
```

profile of v0, /device:TPU:0, one launch (start us, length us, event | category | flops | bytes accessed | tf_op | source)
XLA Modules:
  0.0 254.9 jit_solution(2723518301834246498)
XLA Ops:
  8.0 0.0 copy-start.2
  8.0 0.0 all-reduce.2.cloned.1.call-start
  8.1 0.7 iota_compare_fusion
  8.8 0.1 lt.18
  8.9 2.5 multiply_convert_fusion
  11.4 0.0 copy-start
  11.4 0.0 copy-done.2
  11.4 0.0 copy-start.3
  11.4 0.0 copy-start.1
  11.4 1.8 fusion.1
  13.2 0.0 all-reduce.2.cloned.1.call-update
  13.2 0.0 all-gather.3.cloned.1.call-start
  13.3 0.5 all-gather.3.cloned.1.call-update
  13.8 0.0 all-gather.5.cloned.1.call-start
  13.9 0.0 copy-done
  13.9 0.5 all-gather.5.cloned.1.call-update
  14.4 0.0 copy-done.3
  14.4 219.2 %all-reduce.2.cloned.1.call-done = f32[3072,64]{1,0:T(8,128)} async-done(((f32[3072,64]{1,0:T(8,128)}), f32[3072,64]{1,0:T(8,128)}) %all-reduce.2.cloned.1.call-update) | async-done | bytes 786448 | tf_op jit(solution)/shard_map/psum | solution.py:25
  233.7 0.0 copy-done.1
  233.7 3.5 %convolution_add_fusion = f32[144,64]{0,1:T(8,128)} fusion(bf16[144,3072]{1,0:T(8,128)(2,1)S(1)} %copy-done.1, f32[3072,64]{1,0:T(8,128)} %all-reduce.2.cloned.1.call-done, bf16[144,64]{0,1:T(8,128)(2,1)S(1)} %copy-done.2, f32[144]{0:T(256)S(1)} %broadcast_select_fusion.1), kind=kOutput, calls=%fused_computation.1 | convolution fusion | flops 339766272 | bytes 1727040 | tf_op jit(solution)/shard_map/dot_general | solution.py:26
  237.1 0.0 all-gather.3.cloned.1.call-done
  237.1 0.0 all-gather.5.cloned.1.call-done
  237.1 10.4 %fusion = f32[576,1152]{1,0:T(8,128)} fusion(bf16[576,3072]{1,0:T(8,128)(2,1)} %all-gather.3.cloned.1.call-done, bf16[1152,3072]{1,0:T(8,128)(2,1)} %all-gather.5.cloned.1.call-done), kind=kOutput, calls=%fused_computation.5 | convolution fusion | flops 4076863488 | bytes 13271040 | tf_op jit(solution)/shard_map/dot_general | solution.py:16
  (1 shorter events, 0.0 us)
Async XLA Ops:
  8.0 3.4 %copy-start.2 = (bf16[144,64]{0,1:T(8,128)(2,1)S(1)}, bf16[144,64]{0,1:T(8,128)(2,1)}, u32[]{:S(2)}) copy-start(bf16[144,64]{0,1:T(8,128)(2,1)} %param.9) | copy-start | bytes 55300
  8.0 225.6 %all-reduce.2.cloned.1.call-start = ((), (), s32[]{:S(2)}) async-start(), calls=%async_computation.2 | async-start | bytes 3145728 | tf_op jit(solution)/shard_map/psum | solution.py:25
  11.4 2.5 copy-start
  11.4 3.0 %copy-start.3 = (f32[144]{0:T(256)S(1)}, f32[144]{0:T(256)}, u32[]{:S(2)}) copy-start(f32[144]{0:T(256)} %param.8) | copy-start | bytes 1732
  11.4 222.2 %copy-start.1 = (bf16[144,3072]{1,0:T(8,128)(2,1)S(1)}, bf16[144,3072]{1,0:T(8,128)(2,1)}, u32[]{:S(2)}) copy-start(bf16[144,3072]{1,0:T(8,128)(2,1)} %get-tuple-element.2) | copy-start | bytes 2654212
  13.2 223.9 %all-gather.3.cloned.1.call-start = ((), (), s32[]{:S(2)}) async-start(), calls=%async_computation | async-start | bytes 4423680 | tf_op jit(solution)/shard_map/all_gather | solution.py:15
  13.8 223.3 %all-gather.5.cloned.1.call-start = ((), (), s32[]{:S(2)}) async-start(), calls=%async_computation.1 | async-start | bytes 7962624 | tf_op jit(solution)/shard_map/all_gather | solution.py:18
Sparse Core Ops, SparseCore 0:
  14.7 218.9 all-reduce.1
Sparse Core Ops, SparseCore 1:
  15.3 34.0 all-gather.2
  51.4 109.7 all-gather.4
where the time goes:
time: 255 us
  waiting for transfers between devices  220 us (86%)
  matrix products  15.6 us (6%)
  between operations  15.5 us (6%)
  other arithmetic  3.27 us (1%)
    psum x1, waiting for transfers between devices, body(): projected = lax.psum(local_terms, ('row', 'col'))  219 us
    dot_general x1, matrix products, body(): lax.dot_general(row_block, lax.all_gather(masked, 'row', axis=0, tiled=Tr...  10.4 us
  transfers between devices with their start and end apart: 3, of which 1 were waited for; matrix products, arithmetic and copies ran while one was open for 1% of the time, Pallas kernels for 0%

commit v1 on v0

--- a/solution.py
+++ b/solution.py
@@ -22,7 +22,7 @@
     local_terms = lax.dot_general(
         masked, vectors, (((0,), (0,)), ((), ())), preferred_element_type=jnp.float32
     )
-    projected = lax.psum(local_terms, ("row", "col"))
+    projected = lax.psum(lax.psum(local_terms, "row"), "col")
     coupled = jnp.dot(
         weighted.astype(jnp.float32),
         projected,

time: 255 us -> 309 us (1.21)
  waiting for transfers between devices: 220 us -> 276 us
    all_gather x1, waiting for transfers between devices: 0.01 us -> 110 us  [body(): lax.all_gather(masked, 'row', axis=0, tiled=True)]
    psum x1 -> x2, waiting for transfers between devices: 219 us -> 135 us  [body(): projected = lax.psum(lax.psum(local_terms, 'row'), 'col')]
    all_gather x1, waiting for transfers between devices: 0.01 us -> 28.9 us  [body(): row_block = lax.all_gather(weighted, 'col', axis=0, tiled=True)]
  transfers between devices with their start and end apart: 3 -> 4, of which waited for: 1 -> 4; matrix products, arithmetic and copies ran while one was open for 1% -> 1% of each run, Pallas kernels for 0% -> 0%
where the time goes in v1:
time: 309 us
  waiting for transfers between devices  276 us (89%)
  matrix products  15.6 us (5%)
  between operations  13.8 us (4%)
  other arithmetic  3.17 us (1%)
    psum x2, waiting for transfers between devices, body(): projected = lax.psum(lax.psum(local_terms, 'row'), 'col')  135 us
    all_gather x1, waiting for transfers between devices, body(): lax.all_gather(masked, 'row', axis=0, tiled=True)  110 us
    all_gather x1, waiting for transfers between devices, body(): row_block = lax.all_gather(weighted, 'col', axis=0, tiled=True)  28.9 us
    dot_general x1, matrix products, body(): lax.dot_general(row_block, lax.all_gather(masked, 'row', axis=0, tiled=Tr...  10.4 us
  transfers between devices with their start and end apart: 4, of which 4 were waited for; matrix products, arithmetic and copies ran while one was open for 1% of the time, Pallas kernels for 0%

profile of v1, /device:TPU:0, one launch (start us, length us, event | category | flops | bytes accessed | tf_op | source)
XLA Modules:
  0.0 308.7 jit_solution(5598707812487075882)
XLA Ops:
  7.2 0.0 copy-start.2
  7.2 0.0 all-reduce.3.cloned.1.call-start
  7.2 0.7 iota_compare_fusion
  7.9 0.1 lt.18
  8.0 2.4 multiply_convert_fusion
  10.5 0.0 copy-start
  10.5 0.0 copy-done.2
  10.5 1.8 fusion.1
  12.3 0.0 all-reduce.3.cloned.1.call-update
  12.3 0.0 all-reduce.5.cloned.1.call-start
  12.4 92.1 %all-reduce.3.cloned.1.call-done = f32[3072,64]{1,0:T(8,128)} async-done(((f32[3072,64]{1,0:T(8,128)}), f32[3072,64]{1,0:T(8,128)}) %all-reduce.3.cloned.1.call-update) | async-done | bytes 786448 | tf_op jit(solution)/shard_map/psum | solution.py:25
  104.5 0.0 all-reduce.5.cloned.1.call-update
  104.5 0.0 copy-done
  104.5 0.0 all-gather.3.cloned.1.call-start
  104.6 0.7 all-gather.3.cloned.1.call-update
  105.2 0.0 all-gather.5.cloned.1.call-start
  105.3 0.5 all-gather.5.cloned.1.call-update
  105.8 0.0 copy-done.3
  105.8 43.2 %all-reduce.5.cloned.1.call-done = f32[3072,64]{1,0:T(8,128)} async-done(((f32[3072,64]{1,0:T(8,128)}), f32[3072,64]{1,0:T(8,128)}) %all-reduce.5.cloned.1.call-update) | async-done | bytes 786448 | tf_op jit(solution)/shard_map/psum | solution.py:25
  149.0 0.0 copy-done.1
  149.0 3.5 %convolution_add_fusion = f32[144,64]{0,1:T(8,128)} fusion(bf16[144,3072]{1,0:T(8,128)(2,1)S(1)} %copy-done.1, f32[3072,64]{1,0:T(8,128)} %all-reduce.5.cloned.1.call-done, bf16[144,64]{0,1:T(8,128)(2,1)S(1)} %copy-done.2, f32[144]{0:T(256)S(1)} %broadcast_select_fusion.1), kind=kOutput, calls=%fused_computation.1 | convolution fusion | flops 339766272 | bytes 1727040 | tf_op jit(solution)/shard_map/dot_general | solution.py:26
  152.5 28.9 %all-gather.3.cloned.1.call-done = bf16[576,3072]{1,0:T(8,128)(2,1)} async-done(((bf16[144,3072]{1,0:T(8,128)(2,1)}), bf16[576,3072]{1,0:T(8,128)(2,1)}) %all-gather.3.cloned.1.call-update) | async-done | bytes 3538960 | tf_op jit(solution)/shard_map/all_gather | solution.py:15
  181.4 110.4 %all-gather.5.cloned.1.call-done = bf16[1152,3072]{1,0:T(8,128)(2,1)} async-done(((bf16[144,3072]{1,0:T(8,128)(2,1)}), bf16[1152,3072]{1,0:T(8,128)(2,1)}) %all-gather.5.cloned.1.call-update) | async-done | bytes 7077904 | tf_op jit(solution)/shard_map/all_gather | solution.py:18
  291.8 10.4 %fusion = f32[576,1152]{1,0:T(8,128)} fusion(bf16[576,3072]{1,0:T(8,128)(2,1)} %all-gather.3.cloned.1.call-done, bf16[1152,3072]{1,0:T(8,128)(2,1)} %all-gather.5.cloned.1.call-done), kind=kOutput, calls=%fused_computation.5 | convolution fusion | flops 4076863488 | bytes 13271040 | tf_op jit(solution)/shard_map/dot_general | solution.py:16
  (3 shorter events, 0.0 us)
Async XLA Ops:
  7.2 3.3 %copy-start.2 = (bf16[144,64]{0,1:T(8,128)(2,1)S(1)}, bf16[144,64]{0,1:T(8,128)(2,1)}, u32[]{:S(2)}) copy-start(bf16[144,64]{0,1:T(8,128)(2,1)} %param.9) | copy-start | bytes 55300
  7.2 97.3 %all-reduce.3.cloned.1.call-start = ((), (), s32[]{:S(2)}) async-start(), calls=%async_computation.2 | async-start | bytes 3145728 | tf_op jit(solution)/shard_map/psum | solution.py:25
  10.5 94.0 %copy-start = (bf16[144,3072]{1,0:T(8,128)(2,1)}, bf16[144,3072]{1,0:T(8,128)(2,1)S(1)}, u32[]{:S(2)}) copy-start(bf16[144,3072]{1,0:T(8,128)(2,1)S(1)} %get-tuple-element.3) | copy-start | bytes 2654212
  12.3 93.5 %copy-start.3 = (f32[144]{0:T(256)S(1)}, f32[144]{0:T(256)}, u32[]{:S(2)}) copy-start(f32[144]{0:T(256)} %param.8) | copy-start | bytes 1732
  12.3 136.7 %copy-start.1 = (bf16[144,3072]{1,0:T(8,128)(2,1)S(1)}, bf16[144,3072]{1,0:T(8,128)(2,1)}, u32[]{:S(2)}) copy-start(bf16[144,3072]{1,0:T(8,128)(2,1)} %get-tuple-element.2) | copy-start | bytes 2654212
  12.3 136.7 %all-reduce.5.cloned.1.call-start = ((), (), s32[]{:S(2)}) async-start(), calls=%async_computation.3 | async-start | bytes 3145728 | tf_op jit(solution)/shard_map/psum | solution.py:25
  104.5 76.9 %all-gather.3.cloned.1.call-start = ((), (), s32[]{:S(2)}) async-start(), calls=%async_computation | async-start | bytes 4423680 | tf_op jit(solution)/shard_map/all_gather | solution.py:15
  105.2 186.5 %all-gather.5.cloned.1.call-start = ((), (), s32[]{:S(2)}) async-start(), calls=%async_computation.1 | async-start | bytes 7962624 | tf_op jit(solution)/shard_map/all_gather | solution.py:18
Sparse Core Ops, SparseCore 0:
  12.4 91.9 all-reduce.2
  106.8 42.1 all-reduce.4
  150.6 30.7 all-gather.2
  183.5 108.2 all-gather.4
